TPU v7x, 32 devices: a whole 2x2x4 slice. The times are simulated.
32 devices in a mesh: dp: 8 (over z, y), tensor: 4 (over x, core).
Axes of the slice: x: 2, y: 2, z: 4, core: 2. Of those that a mesh axis runs over, the one named last changes fastest.
Arguments:
- tokens: bfloat16 [16384, 4096], P('dp', 'tensor'), may hold values from -6 to 6
- cotangent: bfloat16 [16384, 1536], P('dp', 'tensor'), may hold values from -0.059814453 to 0.059814453
- seg_start: int32 [8, 2], P('dp'), may hold values from 0 to 1024, as said below
- seg_length: int32 [8, 2], P('dp'), may hold values from 0 to 1024, as said below
Outputs:
- weight_grad: float32 [4096, 2, 1536], P('dp', None, 'tensor')
Inputs may be any that keep to these rules, and one draw needn't show every extreme that they name: Within each index of dp the 2 segments lie in expert order, packed from row 0 without gaps: seg_start is the running sum of seg_length before each expert. `seg_length`: each length is at most 1024; in every draw some expert on some index of dp has exactly 1024 rows. Rows after the last segment belong to no expert.
All inputs are finite; a program needn't handle non-finite values.
Results may differ from a plain program's by a relative error of at most 0.0003.
Values may be sent and summed in bfloat16 or wider, within the bound.
A program may use at most 128 MiB of HBM per device.

v0:
```python
import functools

import jax
import jax.numpy as jnp
from jax import lax
from jax.experimental import pallas as pl
from jax.experimental.pallas import tpu as pltpu
from jax.sharding import PartitionSpec as P

CAP = 1024
SUB = 128
MESH = pl.DeviceIdType.MESH


def block_term(columns, grads, lower, upper, size):
    total_rows = columns.shape[0]
    first = jnp.minimum(lower, total_rows - size)
    rows = first + jnp.arange(size, dtype=jnp.int32)
    keep = (rows >= lower) & (rows < upper)
    block_x = lax.dynamic_slice_in_dim(columns, first, size, 0)
    block_g = lax.dynamic_slice_in_dim(grads, first, size, 0)
    block_g = jnp.where(keep[:, None], block_g, jnp.zeros_like(block_g))
    return lax.dot_general(
        block_x, block_g, (((0,), (0,)), ((), ())), preferred_element_type=jnp.float32
    )


def plain_device(tokens, cotangent, seg_start, seg_length):
    whole = lax.all_gather(tokens, "tensor", axis=1, tiled=True)
    terms = []
    for expert in range(seg_start.shape[1]):
        start = seg_start[0, expert]
        upper = start + seg_length[0, expert]
        terms.append(block_term(whole, cotangent, start, upper, CAP))
    return lax.psum_scatter(jnp.stack(terms, 1), "dp", scatter_dimension=0, tiled=True)


def plan(n_sub, n_ff):
    events = []
    for i in range(max(n_sub, n_ff)):
        events += [("cot", i)] * (i < n_ff) + [("tok", i)] * (i < n_sub)
    groups = []
    for kind, i in events:
        if kind == "tok":
            groups.append((i, []))
    have = {i: max(0, min(n_ff, i + 2)) for i in range(n_sub)}
    seen = set()
    for i, added in groups:
        for j in range(i + 1):
            for f in range(have[i]):
                if (j, f) not in seen:
                    seen.add((j, f))
                    added.append((j, f))
    for j in range(n_sub):
        for f in range(n_ff):
            if (j, f) not in seen:
                groups[-1][1].append((j, f))
    return events, groups, have


def grad_kernel(
    n_dp, n_t, experts, tok_ref, cot_ref, info_ref, out_ref,
    cot_in, info_in, gt, tok, part, recv_r, recv_l,
    tok_send, tok_recv, small_send, small_recv, r_send, r_recv, l_send, l_recv,
):
    d = lax.axis_index("dp")
    t = lax.axis_index("tensor")
    line = n_dp // 2
    z, y = d // 2, d % 2
    rows, width = tok_ref.shape
    ff = cot_ref.shape[1]
    half = width // 2
    n_sub, n_ff = half // SUB, ff // SUB
    n_steps = n_sub * n_ff
    others = n_t // 2 - 1
    partner = (d, t + 1 - 2 * (t % 2))
    pair = (d + 1 - 2 * y, t)
    across = [(d, (t + 2 * k) % n_t) for k in range(1, others + 1)]

    barrier = pltpu.get_barrier_semaphore()
    for device in [partner, pair] + across:
        pl.semaphore_signal(barrier, inc=1, device_id=device, device_id_type=MESH)

    @pl.when(z > 0)
    def _():
        pl.semaphore_signal(barrier, inc=1, device_id=(d - 2, t), device_id_type=MESH)

    @pl.when(z < line - 1)
    def _():
        pl.semaphore_signal(barrier, inc=1, device_id=(d + 2, t), device_id_type=MESH)

    ends = jnp.where(z > 0, 1, 0) + jnp.where(z < line - 1, 1, 0)
    pl.semaphore_wait(barrier, 2 + others + ends)

    def slot(r, j, q):
        return tok.at[r, j, :, pl.ds(pl.multiple_of(q * SUB, SUB), SUB)]

    def own(parity, j):
        return tok_ref.at[:, pl.ds(pl.multiple_of(parity * half + j * SUB, SUB), SUB)]

    def send(src, r, q, j, kind, device):
        return pltpu.make_async_remote_copy(
            src_ref=src, dst_ref=slot(r, j, q), send_sem=tok_send.at[kind, j],
            recv_sem=tok_recv.at[r, q, j], device_id=device, device_id_type=MESH,
        )

    def arrived(r, q, j):
        send(slot(r, j, q), r, q, j, 0, partner).wait_recv()

    info_copy = pltpu.make_async_remote_copy(
        src_ref=info_ref, dst_ref=info_in, send_sem=small_send.at[n_ff],
        recv_sem=small_recv.at[n_ff], device_id=pair, device_id_type=MESH,
    )

    def cot_copy(f):
        at = pl.ds(f * SUB, SUB)
        return pltpu.make_async_remote_copy(
            src_ref=cot_ref.at[:, at], dst_ref=cot_in.at[:, at], send_sem=small_send.at[f],
            recv_sem=small_recv.at[f], device_id=pair, device_id_type=MESH,
        )

    def own_across(j):
        for k, device in enumerate(across):
            send(own(y, j), 0, t, j, 3 + 4 * k, device).start()

    events, groups, have = plan(n_sub, n_ff)
    info_copy.start()
    for kind, i in events:
        if kind == "cot":
            cot_copy(i).start()
        else:
            send(own(1 - y, i), 1, t, i, 1, pair).start()
    for j in range(min(2, n_sub)):
        own_across(j)
    for j in range(n_sub):
        send(own(y, j), 0, t, j, 0, partner).start()
    for j in range(n_sub):
        tok[0, j, :, pl.ds(pl.multiple_of(t * SUB, SUB), SUB)] = tok_ref[
            :, pl.ds(pl.multiple_of(y * half + j * SUB, SUB), SUB)
        ]

    chunk = 256
    deep = experts * SUB

    def masked(r, grads, info, f):
        @pl.loop(0, rows // chunk)
        def _(i):
            at = pl.ds(pl.multiple_of(i * chunk, chunk), chunk)
            block = grads[at, f * SUB : (f + 1) * SUB].astype(jnp.float32).T
            col = i * chunk + lax.broadcasted_iota(jnp.int32, (SUB, chunk), 1)
            for e in range(experts):
                keep = (col >= info[2 * e : 2 * e + 1, :]) & (col < info[2 * e + 1 : 2 * e + 2, :])
                gt[r, f * deep + e * SUB : f * deep + (e + 1) * SUB, at] = jnp.where(
                    keep, block, 0.0
                ).astype(gt.dtype)

    for f in range(n_ff):
        masked(0, cot_ref, info_ref, f)
    info_copy.wait_recv()

    def right(s, q):
        return pltpu.make_async_remote_copy(
            src_ref=part.at[s, q], dst_ref=recv_r.at[s, q], send_sem=r_send.at[s, q],
            recv_sem=r_recv.at[s, q], device_id=(d + 2, t), device_id_type=MESH,
        )

    def left(s, q):
        return pltpu.make_async_remote_copy(
            src_ref=part.at[s, q], dst_ref=recv_l.at[s, q], send_sem=l_send.at[s, q],
            recv_sem=l_recv.at[s, q], device_id=(d - 2, t), device_id_type=MESH,
        )

    def middle(s):
        u, v = s - (z - 1), s - (line - 2 - z)
        for q in reversed(range(n_t)):
            @pl.when((q > z) & (z > 0) & (u >= 0) & (u < n_steps))
            def _():
                right(u, q).wait_recv()
                part[u, q] = part[u, q] + recv_r[u, q]
                right(u, q).start()
        for q in range(n_t):
            @pl.when((q < z) & (z < line - 1) & (v >= 0) & (v < n_steps))
            def _():
                left(v, q).wait_recv()
                part[v, q] = part[v, q] + recv_l[v, q]
                left(v, q).start()

    def from_pair(j):
        arrived(1, t, j)
        for k, device in enumerate(across):
            send(slot(1, j, t), 1, t, j, 4 + 4 * k, device).start()
        send(slot(1, j, t), 1, t, j, 2, partner).start()
        if j + 2 < n_sub:
            own_across(j + 2)

    def from_across(r, j):
        for k in range(others):
            q = (t + 2 * (k + 1)) % n_t
            arrived(r, q, j)
            send(slot(r, j, q), r, q, j, 5 + 4 * k + r, partner).start()

    blocks_in, subs_in, s, hops = 0, 0, 0, 0
    places = []
    last = []
    for i, steps in groups:
        for j in range(subs_in, min(n_sub, i + 1 + (blocks_in == n_ff))):
            while blocks_in < min(n_ff, j + 1):
                cot_copy(blocks_in).wait_recv()
                masked(1, cot_in, info_in, blocks_in)
                blocks_in += 1
            from_pair(j)
            from_across(0, j)
            subs_in = j + 1
        while blocks_in < have[i]:
            cot_copy(blocks_in).wait_recv()
            masked(1, cot_in, info_in, blocks_in)
            blocks_in += 1
        from_across(1, i)
        for r in range(2):
            for k in range(others + 1):
                arrived(r, (partner[1] + 2 * k) % n_t, i)
        for j, f in steps:
            at = pl.ds(f * deep, deep)
            total = jnp.dot(gt[0, at, :], tok[0, j], preferred_element_type=jnp.float32)
            total += jnp.dot(gt[1, at, :], tok[1, j], preferred_element_type=jnp.float32)
            for q in range(n_t):
                part[s, q] = total[:, q * SUB : (q + 1) * SUB]
            for q in range(n_t):
                @pl.when((z == line - 1) & (q < z))
                def _():
                    left(s, q).start()
            for q in reversed(range(n_t)):
                @pl.when((z == 0) & (q > z))
                def _():
                    right(s, q).start()
            places.append((j, f))
            s += 1
        last.append(s)
        if len(last) > 1:
            pl.loop(hops, last[-2])(middle)
            hops = last[-2]
    pl.loop(hops, n_steps + line - 2)(middle)

    for s, (j, f) in enumerate(places):
        here = j * n_ff + f
        out_ref[here] = part[s, z]

        @pl.when(z > 0)
        def _():
            right(s, z).wait_recv()
            out_ref[here] += recv_r[s, z]

        @pl.when(z < line - 1)
        def _():
            left(s, z).wait_recv()
            out_ref[here] += recv_l[s, z]

    @pl.loop(0, n_steps)
    def _(s):
        for q in range(n_t):
            @pl.when(q > z)
            def _():
                right(s, q).wait_send()

            @pl.when(q < z)
            def _():
                left(s, q).wait_send()

    @pl.loop(0, n_sub)
    def _(j):
        for kind in range(3 + 4 * others):
            send(slot(0, j, t), 0, t, j, kind, partner).wait_send()
    for f in range(n_ff):
        cot_copy(f).wait_send()
    info_copy.wait_send()


def kernel_device(n_dp, n_t, tokens, cotangent, seg_start, seg_length):
    rows, width = tokens.shape
    ff = cotangent.shape[1]
    experts = seg_start.shape[1]
    half = width // 2
    n_sub = half // SUB
    others = n_t // 2 - 1
    bounds = jnp.stack([seg_start[0], seg_start[0] + seg_length[0]], 1).reshape(-1)
    pad = -(2 * experts) % 8
    info = jnp.broadcast_to(jnp.pad(bounds, (0, pad))[:, None], (2 * experts + pad, 256))
    dma = pltpu.SemaphoreType.DMA
    n_ff = ff // SUB
    blocks = (n_sub * n_ff, n_t, experts * SUB, SUB)
    vmem = pl.BlockSpec(memory_space=pltpu.VMEM)
    out = pl.pallas_call(
        functools.partial(grad_kernel, n_dp, n_t, experts),
        out_shape=jax.ShapeDtypeStruct((n_sub * n_ff, experts * SUB, SUB), jnp.float32),
        in_specs=[vmem] * 3,
        out_specs=vmem,
        scratch_shapes=[
            pltpu.VMEM((rows, ff), cotangent.dtype),
            pltpu.VMEM(info.shape, jnp.int32),
            pltpu.VMEM((2, experts * ff, rows), cotangent.dtype),
            pltpu.VMEM((2, n_sub, rows, n_t * SUB), tokens.dtype),
            pltpu.VMEM(blocks, jnp.float32),
            pltpu.VMEM(blocks, jnp.float32),
            pltpu.VMEM(blocks, jnp.float32),
            dma((3 + 4 * others, n_sub)),
            dma((2, n_t, n_sub)),
            dma((n_ff + 1,)),
            dma((n_ff + 1,)),
            dma((n_sub * n_ff, n_t)),
            dma((n_sub * n_ff, n_t)),
            dma((n_sub * n_ff, n_t)),
            dma((n_sub * n_ff, n_t)),
        ],
        compiler_params=pltpu.CompilerParams(
            collective_id=0, has_side_effects=True, vmem_limit_bytes=67043328
        ),
    )(tokens, cotangent, info)
    out = out.reshape(n_sub, n_ff, experts, SUB, SUB)
    return out.transpose(0, 4, 2, 1, 3).reshape(half, experts, ff)


def solution(mesh):
    n_dp, n_t = mesh.shape["dp"], mesh.shape["tensor"]
    body = plain_device
    if n_dp == 2 * n_t:
        body = functools.partial(kernel_device, n_dp, n_t)
    in_specs = (P("dp", "tensor"), P("dp", "tensor"), P("dp", None), P("dp", None))
    out_specs = P("dp", None, "tensor")
    return jax.shard_map(
        body, mesh=mesh, in_specs=in_specs, out_specs=out_specs, check_vma=False
    )
```

profile of v0, /device:TPU:0, one launch (start us, length us, event | category | flops | bytes accessed | tf_op | source)
XLA Modules:
  0.0 170.6 jit_solution(14131371801241998590)
XLA Ops:
  0.0 0.7 bitcast_add_fusion
  0.7 0.7 pad_add_fusion
  1.3 0.1 copy.7
  1.4 0.1 reshape.27
  1.5 0.7 broadcast_in_dim.2.info_ref
  2.2 163.3 %shard_map.46 = f32[12,256,128]{2,1,0:T(8,128)} custom-call(bf16[2048,1024]{1,0:T(8,128)(2,1)} %tok_ref.1, bf16[2048,384]{1,0:T(8,128)(2,1)} %cot_ref.1, s32[8,256]{1,0:T(8,128)} %broadcast_in_dim.2.info_ref), custom_call_target="tpu_custom_call" | custom-call | tf_op jit(solution)/shard_map/pallas_call | solution.py:292
  165.5 2.4 %copy.11 = f32[4,3,2,128,128]{4,0,3,1,2:T(4,128)S(1)} copy(f32[4,3,2,128,128]{4,3,2,1,0:T(8,128)} %bitcast.11) | data formatting | bytes 3145728 | tf_op jit(solution)/shard_map/reshape | solution.py:318
  167.9 0.6 reshape.29
  168.5 2.1 %copy.9 = f32[512,2,384]{2,1,0:T(2,128)} copy(f32[512,2,384]{0,2,1:T(8,128)S(1)} %reshape.29) | data formatting | bytes 3145728 | tf_op jit(solution)/shard_map/reshape | solution.py:319
  (1 shorter events, 0.0 us)
where the time goes:
time: 172 us; the launch traced here: 171 us
  Pallas kernels  163 us (95%)
  local copies, waits for them, and re-layouts  5.99 us (3%)
    pallas_call x1, Pallas kernels, kernel_device(): pl.pallas_call(functools.partial(grad_kernel, n_dp, n_t, experts), out_sh...  163 us

commit v1 on v0

v1 whole, which is shorter than its diff:
```python
import functools

import jax
import jax.numpy as jnp
from jax import lax
from jax.experimental import pallas as pl
from jax.experimental.pallas import tpu as pltpu
from jax.sharding import PartitionSpec as P

CAP = 1024
SUB = 128
STEPS = 32767.0
TINY = 1e-30
MESH = pl.DeviceIdType.MESH


def block_term(columns, grads, lower, upper, size):
    total_rows = columns.shape[0]
    first = jnp.minimum(lower, total_rows - size)
    rows = first + jnp.arange(size, dtype=jnp.int32)
    keep = (rows >= lower) & (rows < upper)
    block_x = lax.dynamic_slice_in_dim(columns, first, size, 0)
    block_g = lax.dynamic_slice_in_dim(grads, first, size, 0)
    block_g = jnp.where(keep[:, None], block_g, jnp.zeros_like(block_g))
    return lax.dot_general(
        block_x, block_g, (((0,), (0,)), ((), ())), preferred_element_type=jnp.float32
    )


def plain_device(tokens, cotangent, seg_start, seg_length):
    whole = lax.all_gather(tokens, "tensor", axis=1, tiled=True)
    terms = []
    for expert in range(seg_start.shape[1]):
        start = seg_start[0, expert]
        upper = start + seg_length[0, expert]
        terms.append(block_term(whole, cotangent, start, upper, CAP))
    return lax.psum_scatter(jnp.stack(terms, 1), "dp", scatter_dimension=0, tiled=True)


def unit_order(n_ff):
    if n_ff == 3:
        return [
            (0, 0), (1, 0), (0, 1), (2, 0), (3, 0), (1, 1),
            (2, 1), (3, 1), (1, 2), (2, 2), (3, 2), (0, 2),
        ]
    return [(r, f) for f in range(n_ff) for r in range(4)]


def line_order(units):
    if len(units) == 12:
        return [0, 1, 2, 5, 3, 4, 6, 8, 7, 9, 10, 11]
    return list(range(len(units)))


def pick(values, i):
    found = jnp.int32(values[0])
    for k in range(1, len(values)):
        found = jnp.where(i == k, values[k], found)
    return found


def scaled(value):
    top = jnp.maximum(jnp.max(jnp.abs(value), axis=0, keepdims=True), TINY)
    return jnp.round(value * (STEPS / top)).astype(jnp.int32), top * (1.0 / STEPS)


def grad_kernel(
    n_dp, n_t, experts, tok_ref, cot_ref, start_ref, length_ref, out_ref,
    xv, xt, gbuf, gm, acc, work,
    y_out, y_in, c_out, c_in, z_out, z_in,
    y_out_s, y_in_s, c_out_s, c_in_s, z_out_s, z_in_s,
    load_sem, g_send, g_recv, y_send, y_recv, c_send, c_recv, z_send, z_recv,
):
    d = lax.axis_index("dp")
    t = lax.axis_index("tensor")
    line = n_dp // 2
    z, y = d // 2, d % 2
    x, c = t // 2, t % 2
    rows = cot_ref.shape[0]
    n_ff = gbuf.shape[1]
    half = xv.shape[2]
    tall = half // 2
    units = unit_order(n_ff)
    count = 2 * len(units)
    on_line = line_order(units)
    unit_r = [r for r, f in units]
    unit_f = [f for r, f in units]

    def rel(r):
        return 2 * ((x + r // 2) % 2) + (c + r % 2) % 2

    pair = (d + 1 - 2 * y, t)
    partner, across = (d, rel(1)), (d, rel(2))

    loads = []
    for f in range(n_ff):
        loads.append(pltpu.make_async_copy(
            cot_ref.at[:, pl.ds(f * SUB, SUB)], gbuf.at[0, f], load_sem.at[f]))
    for p, parity in enumerate((1 - y, y)):
        at = pl.ds(pl.multiple_of(parity * half, half), half)
        loads.append(pltpu.make_async_copy(tok_ref.at[:, at], xv.at[p], load_sem.at[n_ff + p]))
    for f in [n_ff, 0] + list(range(1, n_ff)) + [n_ff + 1]:
        loads[f].start()

    barrier = pltpu.get_barrier_semaphore()
    for device in [pair] + [(d, rel(r)) for r in range(1, 4)]:
        pl.semaphore_signal(barrier, inc=1, device_id=device, device_id_type=MESH)

    @pl.when(z > 0)
    def _():
        pl.semaphore_signal(barrier, inc=1, device_id=(d - 2, t), device_id_type=MESH)

    @pl.when(z < line - 1)
    def _():
        pl.semaphore_signal(barrier, inc=1, device_id=(d + 2, t), device_id_type=MESH)

    ends = jnp.where(z > 0, 1, 0) + jnp.where(z < line - 1, 1, 0)
    pl.semaphore_wait(barrier, 4 + ends)

    def remote(src, dst, send, recv, device):
        return pltpu.make_async_remote_copy(
            src_ref=src, dst_ref=dst, send_sem=send, recv_sem=recv,
            device_id=device, device_id_type=MESH,
        )

    def g_copy(r, f):
        if r == 3:
            return remote(gbuf.at[2, f], gbuf.at[3, f], g_send.at[3, f], g_recv.at[3, f], partner)
        src = cot_ref.at[:, pl.ds(f * SUB, SUB)]
        return remote(
            src, gbuf.at[r, f], g_send.at[r, f], g_recv.at[r, f], partner if r == 1 else across)

    for f in range(n_ff):
        g_copy(2, f).start()
        g_copy(1, f).start()

    def y_copies(s):
        return (
            remote(y_out.at[s], y_in.at[s], y_send.at[0, s], y_recv.at[0, s], pair),
            remote(y_out_s.at[s], y_in_s.at[s], y_send.at[1, s], y_recv.at[1, s], pair),
        )

    def c_copies(s, r):
        device = (d, rel(r))
        return (
            remote(c_out.at[s], c_in.at[s], c_send.at[0, s], c_recv.at[0, s], device),
            remote(c_out_s.at[s], c_in_s.at[s], c_send.at[1, s], c_recv.at[1, s], device),
        )

    def z_copies(s, way):
        device = (d + 2 - 4 * way, t)
        return (
            remote(z_out.at[s], z_in.at[way, s], z_send.at[0, s], z_recv.at[way, 0, s], device),
            remote(z_out_s.at[s], z_in_s.at[way, s], z_send.at[1, s], z_recv.at[way, 1, s], device),
        )

    def unscaled(data, scale):
        return data[...].astype(jnp.int32).astype(jnp.float32) * scale[...]

    def put(value, data, scale):
        whole, step = scaled(value)
        data[...] = whole.astype(jnp.int16)
        scale[...] = step

    chunk = 256

    def turn(p):
        @pl.loop(0, rows // chunk)
        def _(i):
            at = pl.ds(pl.multiple_of(i * chunk, chunk), chunk)
            for b in range(half // SUB):
                block = xv[p, at, b * SUB : (b + 1) * SUB].astype(jnp.float32).T
                h, low = b * SUB // tall, b * SUB % tall
                xt[p, h, low : low + SUB, at] = block.astype(xt.dtype)

    loads[n_ff].wait()
    turn(0)

    def form(s):
        u, h = s // 2, s % 2
        r, f = pick(unit_r, u), pick(unit_f, u)

        @pl.when(h == 0)
        def _():
            for k in range(n_ff):
                @pl.when((r == 0) & (f == k))
                def _():
                    loads[k].wait()

                @pl.when((r == 1) & (f == k))
                def _():
                    g_copy(1, k).wait_recv()

                @pl.when((r == 2) & (f == k))
                def _():
                    g_copy(2, k).wait_recv()
                    g_copy(3, k).start()

                @pl.when((r == 3) & (f == k))
                def _():
                    g_copy(3, k).wait_recv()

            @pl.loop(0, rows // chunk)
            def _(i):
                at = pl.ds(pl.multiple_of(i * chunk, chunk), chunk)
                block = gbuf[r, f, at, :].astype(jnp.float32)
                row = i * chunk + lax.broadcasted_iota(jnp.int32, (chunk, SUB), 0)
                for e in range(experts):
                    low = start_ref[0, e]
                    keep = (row >= low) & (row < low + length_ref[0, e])
                    gm[at, e * SUB : (e + 1) * SUB] = jnp.where(keep, block, 0.0).astype(gm.dtype)

        value = jnp.dot(xt[0, h], gm[...], preferred_element_type=jnp.float32)
        put(value, y_out.at[s], y_out_s.at[s])
        for copy in y_copies(s):
            copy.start()

        @pl.when(s == 0)
        def _():
            loads[n_ff + 1].wait()
            turn(1)

        acc[s] = jnp.dot(xt[1, h], gm[...], preferred_element_type=jnp.float32)

    def join(s):
        r = pick(unit_r, s // 2)
        for copy in y_copies(s):
            copy.wait_recv()
        value = acc[s] + unscaled(y_in.at[s], y_in_s.at[s])

        @pl.when(r == 0)
        def _():
            put(value, c_in.at[s], c_in_s.at[s])

        @pl.when(r != 0)
        def _():
            put(value, c_out.at[s], c_out_s.at[s])
            for copy in c_copies(s, r):
                copy.start()

    def at_line(j):
        u = pick(on_line, j // 2)
        r = pick(unit_r, u)
        return 2 * u + j % 2, r, rel(r), pick(unit_f, u)

    def gather(s, r, ways):
        @pl.when(r != 0)
        def _():
            for copy in c_copies(s, r):
                copy.wait_recv()

        work[...] = unscaled(c_in.at[s], c_in_s.at[s])
        for way in ways:
            @pl.when(z > 0 if way == 0 else z < line - 1)
            def _():
                for copy in z_copies(s, way):
                    copy.wait_recv()
                work[...] += unscaled(z_in.at[way, s], z_in_s.at[way, s])

    def pass_on(j, way):
        s, r, to, f = at_line(j)
        further = to > z if way == 0 else to < z

        @pl.when((j >= 0) & (j < count) & further)
        def _():
            gather(s, r, (way,))
            put(work[...], z_out.at[s], z_out_s.at[s])
            for copy in z_copies(s, way):
                copy.start()

    def finish(j):
        s, r, to, f = at_line(j)

        @pl.when((j >= 0) & (j < count) & (to == z))
        def _():
            gather(s, r, (0, 1))
            down = pl.ds(pl.multiple_of((j % 2) * tall, tall), tall)
            along = pl.ds(pl.multiple_of(f * SUB, SUB), SUB)
            for e in range(experts):
                out_ref[e, down, along] = work[:, e * SUB : (e + 1) * SUB]

    JOIN, LINE, HOP = 4, 9, 2

    @pl.loop(0, count + LINE + HOP * (line - 1))
    def _(i):
        @pl.when(i < count)
        def _():
            form(i)

        @pl.when((i >= JOIN) & (i < count + JOIN))
        def _():
            join(i - JOIN)

        pass_on(i - LINE - HOP * z, 0)
        pass_on(i - LINE - HOP * (line - 1 - z), 1)
        finish(i - LINE - HOP * jnp.maximum(z, line - 1 - z))

    @pl.loop(0, count)
    def _(s):
        r = pick(unit_r, s // 2)
        to = rel(r)
        for copy in y_copies(s):
            copy.wait_send()

        @pl.when(r != 0)
        def _():
            for copy in c_copies(s, r):
                copy.wait_send()

        for way in range(2):
            @pl.when(to > z if way == 0 else to < z)
            def _():
                for copy in z_copies(s, way):
                    copy.wait_send()

    for f in range(n_ff):
        for r in range(1, 4):
            g_copy(r, f).wait_send()


def kernel_device(n_dp, n_t, tokens, cotangent, seg_start, seg_length):
    rows, width = tokens.shape
    ff = cotangent.shape[1]
    experts = seg_start.shape[1]
    half = width // 2
    tall = half // 2
    n_ff = ff // SUB
    count = 2 * n_t * n_ff
    wide = experts * SUB
    dma = pltpu.SemaphoreType.DMA
    anywhere = pl.BlockSpec(memory_space=pl.ANY)
    scalars = pl.BlockSpec(memory_space=pltpu.SMEM)
    data = pltpu.VMEM((count, tall, wide), jnp.int16)
    scale = pltpu.VMEM((count, 1, wide), jnp.float32)
    out = pl.pallas_call(
        functools.partial(grad_kernel, n_dp, n_t, experts),
        out_shape=jax.ShapeDtypeStruct((experts, half, ff), jnp.float32),
        in_specs=[anywhere, anywhere, scalars, scalars],
        out_specs=pl.BlockSpec(memory_space=pltpu.VMEM),
        scratch_shapes=[
            pltpu.VMEM((2, rows, half), tokens.dtype),
            pltpu.VMEM((2, 2, tall, rows), tokens.dtype),
            pltpu.VMEM((n_t, n_ff, rows, SUB), cotangent.dtype),
            pltpu.VMEM((rows, wide), cotangent.dtype),
            pltpu.VMEM((count, tall, wide), jnp.float32),
            pltpu.VMEM((tall, wide), jnp.float32),
            data, data, data, data, data,
            pltpu.VMEM((2, count, tall, wide), jnp.int16),
            scale, scale, scale, scale, scale,
            pltpu.VMEM((2, count, 1, wide), jnp.float32),
            dma((n_ff + 2,)),
            dma((n_t, n_ff)),
            dma((n_t, n_ff)),
            dma((2, count)),
            dma((2, count)),
            dma((2, count)),
            dma((2, count)),
            dma((2, count)),
            dma((2, 2, count)),
        ],
        compiler_params=pltpu.CompilerParams(
            collective_id=0, has_side_effects=True, vmem_limit_bytes=67043328
        ),
    )(tokens, cotangent, seg_start, seg_length)
    return out.transpose(1, 0, 2)


def solution(mesh):
    n_dp, n_t = mesh.shape["dp"], mesh.shape["tensor"]
    body = plain_device
    if n_t == 4 and n_dp == 2 * n_t:
        body = functools.partial(kernel_device, n_dp, n_t)
    in_specs = (P("dp", "tensor"), P("dp", "tensor"), P("dp", None), P("dp", None))
    out_specs = P("dp", None, "tensor")
    return jax.shard_map(
        body, mesh=mesh, in_specs=in_specs, out_specs=out_specs, check_vma=False
    )
```

time: 172 us -> 113 us (0.66)
  Pallas kernels: 163 us -> 110 us
  local copies, waits for them, and re-layouts: 5.99 us -> 3.76 us
    pallas_call x1, Pallas kernels: 163 us -> 110 us  [kernel_device(): pl.pallas_call(functools.partial(grad_kernel, n_dp, n_t, experts), out_sh...]
    reshape x4 -> x0, local copies, waits for them, and re-layouts: 5.22 us -> none  [the longest x2 2.71 us: kernel_device(): return out.transpose(0, 4, 2, 1, 3).reshape(half, experts, ff)]
    transpose x0 -> x1, local copies, waits for them, and re-layouts: none -> 3.76 us  [kernel_device(): return out.transpose(1, 0, 2)]
where the time goes in v1:
time: 113 us
  Pallas kernels  110 us (97%)
  local copies, waits for them, and re-layouts  3.76 us (3%)
    pallas_call x1, Pallas kernels, kernel_device(): pl.pallas_call(functools.partial(grad_kernel, n_dp, n_t, experts), out_sh...  110 us
    transpose x1, local copies, waits for them, and re-layouts, kernel_device(): return out.transpose(1, 0, 2)  3.76 us

profile of v1, /device:TPU:0, one launch (start us, length us, event | category | flops | bytes accessed | tf_op | source)
XLA Modules:
  0.0 113.3 jit_solution(4177818675076777919)
XLA Ops:
  0.0 109.5 %shard_map.46 = f32[2,512,384]{2,1,0:T(8,128)} custom-call(bf16[2048,1024]{1,0:T(8,128)(2,1)} %tok_ref.1, bf16[2048,384]{1,0:T(8,128)(2,1)} %cot_ref.1, s32[1,2]{1,0:T(1,128)} %start_ref.1, s32[1,2]{1,0:T(1,128)} %length_ref.1), custom_call_target="tpu_custom_call" | custom-call | tf_op jit(solution)/shard_map/pallas_call | solution.py:335
  109.5 3.8 %copy.5 = f32[512,2,384]{2,1,0:T(2,128)} copy(f32[512,2,384]{2,0,1:T(8,128)} %bitcast.1) | data formatting | bytes 3145728 | tf_op jit(solution)/shard_map/transpose | solution.py:365

commit v2 on v1

v2 whole, which is shorter than its diff:
```python
import functools

import jax
import jax.numpy as jnp
from jax import lax
from jax.experimental import pallas as pl
from jax.experimental.pallas import tpu as pltpu
from jax.sharding import PartitionSpec as P

CAP = 1024
SUB = 128
STEPS = 32767.0
TINY = 1e-30
JOIN, MERGE, LAST = 4, 2, 5
MESH = pl.DeviceIdType.MESH


def block_term(columns, grads, lower, upper, size):
    total_rows = columns.shape[0]
    first = jnp.minimum(lower, total_rows - size)
    rows = first + jnp.arange(size, dtype=jnp.int32)
    keep = (rows >= lower) & (rows < upper)
    block_x = lax.dynamic_slice_in_dim(columns, first, size, 0)
    block_g = lax.dynamic_slice_in_dim(grads, first, size, 0)
    block_g = jnp.where(keep[:, None], block_g, jnp.zeros_like(block_g))
    return lax.dot_general(
        block_x, block_g, (((0,), (0,)), ((), ())), preferred_element_type=jnp.float32
    )


def plain_device(tokens, cotangent, seg_start, seg_length):
    whole = lax.all_gather(tokens, "tensor", axis=1, tiled=True)
    terms = []
    for expert in range(seg_start.shape[1]):
        start = seg_start[0, expert]
        upper = start + seg_length[0, expert]
        terms.append(block_term(whole, cotangent, start, upper, CAP))
    return lax.psum_scatter(jnp.stack(terms, 1), "dp", scatter_dimension=0, tiled=True)


def unit_order(n_ff):
    if n_ff == 3:
        return [
            (0, 0), (1, 0), (1, 1), (1, 2), (2, 0), (3, 0),
            (2, 1), (3, 1), (2, 2), (3, 2), (0, 1), (0, 2),
        ]
    return [(r, f) for f in range(n_ff) for r in range(4)]


def pick(values, i):
    found = jnp.int32(values[0])
    for k in range(1, len(values)):
        found = jnp.where(i == k, values[k], found)
    return found


def grad_kernel(
    n_dp, n_t, experts, tok_ref, cot_ref, start_ref, length_ref, out_ref,
    xv, xt, gbuf, gm, acc, fresh, result, y_out, y_in, w_out, w_in,
    y_out_s, y_in_s, w_out_s, w_in_s,
    load_sem, g_send, g_recv, y_send, y_recv, w_send, w_recv, f_send, f_recv, store_sem,
):
    d = lax.axis_index("dp")
    t = lax.axis_index("tensor")
    line = n_dp // 2
    z, y = d // 2, d % 2
    x, c = t // 2, t % 2
    rows = cot_ref.shape[0]
    n_ff = gbuf.shape[1]
    tall = xv.shape[3]
    half = 2 * tall
    units = unit_order(n_ff)
    count = 2 * len(units)
    unit_r = [r for r, f in units]
    unit_f = [f for r, f in units]

    def unit_of(s):
        return 2 * (s // 4) + s % 2

    def rel(r):
        return 2 * ((x + r // 2) % 2) + (c + r % 2) % 2

    pair = (d + 1 - 2 * y, t)
    partner, across = (d, rel(1)), (d, rel(2))

    loads = {}
    for f in range(n_ff):
        loads[f] = pltpu.make_async_copy(
            cot_ref.at[:, pl.ds(f * SUB, SUB)], gbuf.at[0, f], load_sem.at[f])
    for p, parity in enumerate((1 - y, y)):
        for h in range(2):
            at = pl.ds(pl.multiple_of(parity * half + h * tall, tall), tall)
            loads[p, h] = pltpu.make_async_copy(
                tok_ref.at[:, at], xv.at[p, h], load_sem.at[n_ff + 2 * p + h])
    for name in [(0, 0), 0, (1, 0), (0, 1), (1, 1)] + list(range(1, n_ff)):
        loads[name].start()

    barrier = pltpu.get_barrier_semaphore()
    others = [(2 * ((z + k) % line) + y, t) for k in range(1, line)]
    for device in [pair] + [(d, rel(r)) for r in range(1, 4)] + others:
        pl.semaphore_signal(barrier, inc=1, device_id=device, device_id_type=MESH)
    pl.semaphore_wait(barrier, 4 + len(others))

    target = z == t
    merger = ((z == 1) & (t >= 2)) | ((z == 2) & (t <= 1))
    feeder = ((z != t) & (z != 1) & (z != 2)) | ((z == 1) & (t == 0)) | ((z == 2) & (t == 3))
    plane = jnp.where(feeder & (z == 0), 1, jnp.where(feeder & (z == line - 1), 2, t))

    def remote(src, dst, send, recv, device):
        return pltpu.make_async_remote_copy(
            src_ref=src, dst_ref=dst, send_sem=send, recv_sem=recv,
            device_id=device, device_id_type=MESH,
        )

    def g_copy(r, f):
        if r == 3:
            return remote(gbuf.at[2, f], gbuf.at[3, f], g_send.at[3, f], g_recv.at[3, f], partner)
        src = cot_ref.at[:, pl.ds(f * SUB, SUB)]
        return remote(
            src, gbuf.at[r, f], g_send.at[r, f], g_recv.at[r, f], partner if r == 1 else across)

    for f in range(n_ff):
        g_copy(2, f).start()
        g_copy(1, f).start()

    def y_copies(s):
        return (
            remote(y_out.at[s], y_in.at[s], y_send.at[0, s], y_recv.at[0, s], pair),
            remote(y_out_s.at[s], y_in_s.at[s], y_send.at[1, s], y_recv.at[1, s], pair),
        )

    def w_copies(s, way):
        device = (2 * plane + y, t)
        return (
            remote(w_out.at[s], w_in.at[way, s], w_send.at[0, s], w_recv.at[way, 0, s], device),
            remote(w_out_s.at[s], w_in_s.at[way, s], w_send.at[1, s], w_recv.at[way, 1, s], device),
        )

    def place(f, h, e):
        down = pl.ds(h * tall, tall)
        along = pl.ds(pl.multiple_of(f * SUB, SUB), SUB)
        return e, down, along

    def f_copies(s, r, f, h):
        return [
            remote(
                acc.at[s, :, pl.ds(e * SUB, SUB)], result.at[place(f, h, e)],
                f_send.at[s, e], f_recv.at[f, h, e], (d, rel(r)))
            for e in range(experts)
        ]

    def stores(f, h):
        return [
            pltpu.make_async_copy(
                result.at[place(f, h, e)], out_ref.at[place(f, h, e)], store_sem.at[f, h, e])
            for e in range(experts)
        ]

    chunk = 256
    part = tall // 4

    def unscaled(data, scale, at):
        return data[at, :].astype(jnp.int32).astype(jnp.float32) * scale[...]

    def highest(top, value):
        return jnp.maximum(top, jnp.max(jnp.abs(value), axis=0, keepdims=True))

    def put(value, top, data, scale):
        top = jnp.maximum(top, TINY)
        factor = STEPS / top
        scale[...] = top * (1.0 / STEPS)
        for k in range(4):
            at = pl.ds(k * part, part)
            whole = jnp.round(value[at, :] * factor).astype(jnp.int32)
            data[at, :] = whole.astype(jnp.int16)

    def turn(p, h):
        loads[p, h].wait()

        @pl.loop(0, rows // chunk)
        def _(i):
            at = pl.ds(pl.multiple_of(i * chunk, chunk), chunk)
            for b in range(tall // SUB):
                block = xv[p, h, at, b * SUB : (b + 1) * SUB].astype(jnp.float32).T
                xt[p, h, b * SUB : (b + 1) * SUB, at] = block.astype(xt.dtype)

    def arrive(r, f):
        for k in range(n_ff):
            @pl.when((r == 0) & (f == k))
            def _():
                loads[k].wait()

            @pl.when((r == 1) & (f == k))
            def _():
                g_copy(1, k).wait_recv()

            @pl.when((r == 2) & (f == k))
            def _():
                g_copy(2, k).wait_recv()
                g_copy(3, k).start()

            @pl.when((r == 3) & (f == k))
            def _():
                g_copy(3, k).wait_recv()

    def product(p, h, into):
        for e in range(experts):
            deep = rows * (e + 1) // experts
            value = jnp.dot(
                xt[p, h, :, :deep], gm[:deep, 2 * e * SUB : 2 * (e + 1) * SUB],
                preferred_element_type=jnp.float32,
            )
            for a in range(2):
                into[a, :, e * SUB : (e + 1) * SUB] = value[:, a * SUB : (a + 1) * SUB]

    def form(s):
        k, h = s // 4, (s // 2) % 2

        @pl.when(h == 0)
        def _():
            for a in range(2):
                r, f = pick(unit_r, 2 * k + a), pick(unit_f, 2 * k + a)
                arrive(r, f)
                for e in range(experts):
                    low = start_ref[0, e]
                    high = low + length_ref[0, e]

                    @pl.loop(0, rows * (e + 1) // experts // chunk)
                    def _(i):
                        at = pl.ds(pl.multiple_of(i * chunk, chunk), chunk)
                        block = gbuf[r, f, at, :].astype(jnp.float32)
                        row = i * chunk + lax.broadcasted_iota(jnp.int32, (chunk, SUB), 0)
                        keep = (row >= low) & (row < high)
                        gm[at, (2 * e + a) * SUB : (2 * e + a + 1) * SUB] = jnp.where(
                            keep, block, 0.0
                        ).astype(gm.dtype)

        for step in range(2):
            @pl.when(s == 2 * step)
            def _():
                turn(0, step)

        product(0, h, fresh)
        for a in range(2):
            put(fresh.at[a], highest(0.0, fresh[a]), y_out.at[s + a], y_out_s.at[s + a])
            for copy in y_copies(s + a):
                copy.start()

        for step in range(2):
            @pl.when(s == 2 * step)
            def _():
                turn(1, step)

        product(1, h, acc.at[pl.ds(s, 2)])

    def settle(s, sources):
        h = (s // 2) % 2
        r, f = pick(unit_r, unit_of(s)), pick(unit_f, unit_of(s))
        for copy in y_copies(s):
            copy.wait_recv()
        for way in range(sources):
            for copy in w_copies(s, way):
                copy.wait_recv()
        top = jnp.zeros((1, acc.shape[2]), jnp.float32)
        for k in range(4):
            at = pl.ds(k * part, part)
            value = acc[s, at, :] + unscaled(y_in.at[s], y_in_s.at[s], at)
            for way in range(sources):
                value += unscaled(w_in.at[way, s], w_in_s.at[way, s], at)
            acc[s, at, :] = value
            if sources < 2:
                top = highest(top, value)
        if sources < 2:
            put(acc.at[s], top, w_out.at[s], w_out_s.at[s])
            for copy in w_copies(s, sources):
                copy.start()
            return

        @pl.when(r == 0)
        def _():
            for e in range(experts):
                result[place(f, h, e)] = acc[s, :, e * SUB : (e + 1) * SUB]
            for copy in stores(f, h):
                copy.start()

        @pl.when(r != 0)
        def _():
            for copy in f_copies(s, r, f, h):
                copy.start()

    lags = (JOIN, JOIN + MERGE, JOIN + LAST)

    @pl.loop(0, count + lags[2])
    def _(i):
        @pl.when((i < count) & (i % 2 == 0))
        def _():
            form(i)

        for sources, role in enumerate((feeder, merger, target)):
            @pl.when(role & (i >= lags[sources]) & (i < count + lags[sources]))
            def _():
                settle(i - lags[sources], sources)

    blocks = [(f, h) for f in range(n_ff) for h in range(2)]

    @pl.when(z != t)
    def _():
        for f, h in blocks:
            for e, copy in enumerate(f_copies(0, 1, f, h)):
                copy.wait_recv()
            for copy in stores(f, h):
                copy.start()

    @pl.loop(0, count)
    def _(s):
        r = pick(unit_r, unit_of(s))
        for copy in y_copies(s):
            copy.wait_send()

        @pl.when(z != t)
        def _():
            for copy in w_copies(s, 0):
                copy.wait_send()

        @pl.when((z == t) & (r != 0))
        def _():
            for copy in f_copies(s, r, 0, 0):
                copy.wait_send()

    for f in range(n_ff):
        for r in range(1, 4):
            g_copy(r, f).wait_send()
    for f, h in blocks:
        for copy in stores(f, h):
            copy.wait()


def kernel_device(n_dp, n_t, tokens, cotangent, seg_start, seg_length):
    rows, width = tokens.shape
    ff = cotangent.shape[1]
    experts = seg_start.shape[1]
    half = width // 2
    tall = half // 2
    n_ff = ff // SUB
    count = 2 * n_t * n_ff
    wide = experts * SUB
    dma = pltpu.SemaphoreType.DMA
    anywhere = pl.BlockSpec(memory_space=pl.ANY)
    scalars = pl.BlockSpec(memory_space=pltpu.SMEM)
    data = pltpu.VMEM((count, tall, wide), jnp.int16)
    scale = pltpu.VMEM((count, 1, wide), jnp.float32)
    out = pl.pallas_call(
        functools.partial(grad_kernel, n_dp, n_t, experts),
        out_shape=jax.ShapeDtypeStruct((experts, half, ff), jnp.float32),
        in_specs=[anywhere, anywhere, scalars, scalars],
        out_specs=anywhere,
        scratch_shapes=[
            pltpu.VMEM((2, 2, rows, tall), tokens.dtype),
            pltpu.VMEM((2, 2, tall, rows), tokens.dtype),
            pltpu.VMEM((n_t, n_ff, rows, SUB), cotangent.dtype),
            pltpu.VMEM((rows, 2 * wide), cotangent.dtype),
            pltpu.VMEM((count, tall, wide), jnp.float32),
            pltpu.VMEM((2, tall, wide), jnp.float32),
            pltpu.VMEM((experts, half, ff), jnp.float32),
            data, data, data,
            pltpu.VMEM((2, count, tall, wide), jnp.int16),
            scale, scale, scale,
            pltpu.VMEM((2, count, 1, wide), jnp.float32),
            dma((n_ff + 4,)),
            dma((n_t, n_ff)),
            dma((n_t, n_ff)),
            dma((2, count)),
            dma((2, count)),
            dma((2, count)),
            dma((2, 2, count)),
            dma((count, experts)),
            dma((n_ff, 2, experts)),
            dma((n_ff, 2, experts)),
        ],
        compiler_params=pltpu.CompilerParams(
            collective_id=0, has_side_effects=True, vmem_limit_bytes=67043328
        ),
    )(tokens, cotangent, seg_start, seg_length)
    return out.transpose(1, 0, 2)


def solution(mesh):
    n_dp, n_t = mesh.shape["dp"], mesh.shape["tensor"]
    body = plain_device
    if n_t == 4 and n_dp == 2 * n_t:
        body = functools.partial(kernel_device, n_dp, n_t)
    in_specs = (P("dp", "tensor"), P("dp", "tensor"), P("dp", None), P("dp", None))
    out_specs = P("dp", None, "tensor")
    return jax.shard_map(
        body, mesh=mesh, in_specs=in_specs, out_specs=out_specs, check_vma=False
    )
```

time: 113 us -> 103 us (0.912)
  Pallas kernels: 110 us -> 98.9 us
    pallas_call x1, Pallas kernels: 110 us -> 98.9 us  [kernel_device(): pl.pallas_call(functools.partial(grad_kernel, n_dp, n_t, experts), out_sh...]
where the time goes in v2:
time: 103 us
  Pallas kernels  98.9 us (96%)
  local copies, waits for them, and re-layouts  3.76 us (4%)
    pallas_call x1, Pallas kernels, kernel_device(): pl.pallas_call(functools.partial(grad_kernel, n_dp, n_t, experts), out_sh...  98.9 us
    transpose x1, local copies, waits for them, and re-layouts, kernel_device(): return out.transpose(1, 0, 2)  3.76 us

profile of v2, /device:TPU:0, one launch (start us, length us, event | category | flops | bytes accessed | tf_op | source)
XLA Modules:
  0.0 102.6 jit_solution(1400678000899431020)
XLA Ops:
  0.0 98.9 %shard_map.46 = f32[2,512,384]{2,1,0:T(8,128)} custom-call(bf16[2048,1024]{1,0:T(8,128)(2,1)} %tok_ref.1, bf16[2048,384]{1,0:T(8,128)(2,1)} %cot_ref.1, s32[1,2]{1,0:T(1,128)} %start_ref.1, s32[1,2]{1,0:T(1,128)} %length_ref.1), custom_call_target="tpu_custom_call" | custom-call | tf_op jit(solution)/shard_map/pallas_call | solution.py:352
  98.9 3.8 %copy.5 = f32[512,2,384]{2,1,0:T(2,128)} copy(f32[512,2,384]{2,0,1:T(8,128)} %bitcast.1) | data formatting | bytes 3145728 | tf_op jit(solution)/shard_map/transpose | solution.py:384

commit v3 on v2

--- a/solution.py
+++ b/solution.py
@@ -11,7 +11,7 @@
 SUB = 128
 STEPS = 32767.0
 TINY = 1e-30
-JOIN, MERGE, LAST = 4, 2, 5
+JOIN, MERGE, LAST = 2, 2, 5
 MESH = pl.DeviceIdType.MESH
 
 
@@ -41,8 +41,8 @@
 def unit_order(n_ff):
     if n_ff == 3:
         return [
-            (0, 0), (1, 0), (1, 1), (1, 2), (2, 0), (3, 0),
-            (2, 1), (3, 1), (2, 2), (3, 2), (0, 1), (0, 2),
+            (0, 0), (0, 1), (1, 0), (1, 1), (2, 0), (3, 0),
+            (2, 1), (3, 1), (2, 2), (3, 2), (1, 2), (0, 2),
         ]
     return [(r, f) for f in range(n_ff) for r in range(4)]
 
@@ -92,14 +92,13 @@
             at = pl.ds(pl.multiple_of(parity * half + h * tall, tall), tall)
             loads[p, h] = pltpu.make_async_copy(
                 tok_ref.at[:, at], xv.at[p, h], load_sem.at[n_ff + 2 * p + h])
-    for name in [(0, 0), 0, (1, 0), (0, 1), (1, 1)] + list(range(1, n_ff)):
+    for name in [(0, 0), 0, 1, (1, 0), (0, 1), (1, 1)] + list(range(2, n_ff)):
         loads[name].start()
 
     barrier = pltpu.get_barrier_semaphore()
     others = [(2 * ((z + k) % line) + y, t) for k in range(1, line)]
     for device in [pair] + [(d, rel(r)) for r in range(1, 4)] + others:
         pl.semaphore_signal(barrier, inc=1, device_id=device, device_id_type=MESH)
-    pl.semaphore_wait(barrier, 4 + len(others))
 
     target = z == t
     merger = ((z == 1) & (t >= 2)) | ((z == 2) & (t <= 1))
@@ -118,10 +117,6 @@
         src = cot_ref.at[:, pl.ds(f * SUB, SUB)]
         return remote(
             src, gbuf.at[r, f], g_send.at[r, f], g_recv.at[r, f], partner if r == 1 else across)
-
-    for f in range(n_ff):
-        g_copy(2, f).start()
-        g_copy(1, f).start()
 
     def y_copies(s):
         return (
@@ -181,7 +176,7 @@
         def _(i):
             at = pl.ds(pl.multiple_of(i * chunk, chunk), chunk)
             for b in range(tall // SUB):
-                block = xv[p, h, at, b * SUB : (b + 1) * SUB].astype(jnp.float32).T
+                block = xv[p, h, at, b * SUB : (b + 1) * SUB].T
                 xt[p, h, b * SUB : (b + 1) * SUB, at] = block.astype(xt.dtype)
 
     def arrive(r, f):
@@ -213,36 +208,45 @@
             for a in range(2):
                 into[a, :, e * SUB : (e + 1) * SUB] = value[:, a * SUB : (a + 1) * SUB]
 
+    def cover(r, f, a):
+        for e in range(experts):
+            low = start_ref[0, e]
+            high = low + length_ref[0, e]
+
+            @pl.loop(0, rows * (e + 1) // experts // chunk)
+            def _(i):
+                at = pl.ds(pl.multiple_of(i * chunk, chunk), chunk)
+                block = gbuf[r, f, at, :].astype(jnp.float32)
+                row = i * chunk + lax.broadcasted_iota(jnp.int32, (chunk, SUB), 0)
+                keep = (row >= low) & (row < high)
+                gm[at, (2 * e + a) * SUB : (2 * e + a + 1) * SUB] = jnp.where(
+                    keep, block, 0.0
+                ).astype(gm.dtype)
+
+    def ready(s, h):
+        product(0, h, fresh)
+        for a in range(2):
+            put(fresh.at[a], highest(0.0, fresh[a]), y_out.at[s + a], y_out_s.at[s + a])
+
     def form(s):
         k, h = s // 4, (s // 2) % 2
 
-        @pl.when(h == 0)
+        @pl.when((h == 0) & (s > 0))
         def _():
             for a in range(2):
                 r, f = pick(unit_r, 2 * k + a), pick(unit_f, 2 * k + a)
                 arrive(r, f)
-                for e in range(experts):
-                    low = start_ref[0, e]
-                    high = low + length_ref[0, e]
-
-                    @pl.loop(0, rows * (e + 1) // experts // chunk)
-                    def _(i):
-                        at = pl.ds(pl.multiple_of(i * chunk, chunk), chunk)
-                        block = gbuf[r, f, at, :].astype(jnp.float32)
-                        row = i * chunk + lax.broadcasted_iota(jnp.int32, (chunk, SUB), 0)
-                        keep = (row >= low) & (row < high)
-                        gm[at, (2 * e + a) * SUB : (2 * e + a + 1) * SUB] = jnp.where(
-                            keep, block, 0.0
-                        ).astype(gm.dtype)
-
-        for step in range(2):
-            @pl.when(s == 2 * step)
-            def _():
-                turn(0, step)
-
-        product(0, h, fresh)
+                cover(r, f, a)
+
+        @pl.when(s == 2)
+        def _():
+            turn(0, 1)
+
+        @pl.when(s > 0)
+        def _():
+            ready(s, h)
+
         for a in range(2):
-            put(fresh.at[a], highest(0.0, fresh[a]), y_out.at[s + a], y_out_s.at[s + a])
             for copy in y_copies(s + a):
                 copy.start()
 
@@ -287,6 +291,16 @@
         def _():
             for copy in f_copies(s, r, f, h):
                 copy.start()
+
+    turn(0, 0)
+    for a in range(2):
+        loads[units[a][1]].wait()
+        cover(*units[a], a)
+    ready(0, 0)
+    pl.semaphore_wait(barrier, 4 + len(others))
+    for f in range(n_ff):
+        g_copy(2, f).start()
+        g_copy(1, f).start()
 
     lags = (JOIN, JOIN + MERGE, JOIN + LAST)
 

time: 103 us -> 97.8 us (0.950)
  Pallas kernels: 98.9 us -> 93.9 us
    pallas_call x1, Pallas kernels: 98.9 us -> 93.9 us  [kernel_device(): pl.pallas_call(functools.partial(grad_kernel, n_dp, n_t, experts), out_sh...]
where the time goes in v3:
time: 97.8 us; the launch traced here: 97.6 us
  Pallas kernels  93.9 us (96%)
  local copies, waits for them, and re-layouts  3.76 us (4%)
    pallas_call x1, Pallas kernels, kernel_device(): pl.pallas_call(functools.partial(grad_kernel, n_dp, n_t, experts), out_sh...  93.9 us
    transpose x1, local copies, waits for them, and re-layouts, kernel_device(): return out.transpose(1, 0, 2)  3.76 us

profile of v3, /device:TPU:0, one launch (start us, length us, event | category | flops | bytes accessed | tf_op | source)
XLA Modules:
  0.0 97.6 jit_solution(6934899403908626958)
XLA Ops:
  0.0 93.9 %shard_map.46 = f32[2,512,384]{2,1,0:T(8,128)} custom-call(bf16[2048,1024]{1,0:T(8,128)(2,1)} %tok_ref.1, bf16[2048,384]{1,0:T(8,128)(2,1)} %cot_ref.1, s32[1,2]{1,0:T(1,128)} %start_ref.1, s32[1,2]{1,0:T(1,128)} %length_ref.1), custom_call_target="tpu_custom_call" | custom-call | tf_op jit(solution)/shard_map/pallas_call | solution.py:366
  93.9 3.8 %copy.5 = f32[512,2,384]{2,1,0:T(2,128)} copy(f32[512,2,384]{2,0,1:T(8,128)} %bitcast.1) | data formatting | bytes 3145728 | tf_op jit(solution)/shard_map/transpose | solution.py:398

commit v4 on v3

--- a/solution.py
+++ b/solution.py
@@ -11,7 +11,7 @@
 SUB = 128
 STEPS = 32767.0
 TINY = 1e-30
-JOIN, MERGE, LAST = 2, 2, 5
+JOIN, MERGE, LAST = 4, 1, 3
 MESH = pl.DeviceIdType.MESH
 
 
@@ -55,10 +55,11 @@
 
 
 def grad_kernel(
-    n_dp, n_t, experts, tok_ref, cot_ref, start_ref, length_ref, out_ref,
+    n_dp, n_t, experts, tok_ref, cot_ref, start_hbm, length_hbm, out_ref,
     xv, xt, gbuf, gm, acc, fresh, result, y_out, y_in, w_out, w_in,
     y_out_s, y_in_s, w_out_s, w_in_s,
     load_sem, g_send, g_recv, y_send, y_recv, w_send, w_recv, f_send, f_recv, store_sem,
+    start_ref, length_ref, seg_sem,
 ):
     d = lax.axis_index("dp")
     t = lax.axis_index("tensor")
@@ -94,6 +95,12 @@
                 tok_ref.at[:, at], xv.at[p, h], load_sem.at[n_ff + 2 * p + h])
     for name in [(0, 0), 0, 1, (1, 0), (0, 1), (1, 1)] + list(range(2, n_ff)):
         loads[name].start()
+    segments = [
+        pltpu.make_async_copy(start_hbm, start_ref, seg_sem.at[0]),
+        pltpu.make_async_copy(length_hbm, length_ref, seg_sem.at[1]),
+    ]
+    for copy in segments:
+        copy.start()
 
     barrier = pltpu.get_barrier_semaphore()
     others = [(2 * ((z + k) % line) + y, t) for k in range(1, line)]
@@ -118,11 +125,12 @@
         return remote(
             src, gbuf.at[r, f], g_send.at[r, f], g_recv.at[r, f], partner if r == 1 else across)
 
-    def y_copies(s):
-        return (
-            remote(y_out.at[s], y_in.at[s], y_send.at[0, s], y_recv.at[0, s], pair),
-            remote(y_out_s.at[s], y_in_s.at[s], y_send.at[1, s], y_recv.at[1, s], pair),
-        )
+    def y_copy(s):
+        return remote(y_out.at[s], y_in.at[s], y_send.at[0, s], y_recv.at[0, s], pair)
+
+    def y_scale(s):
+        at = pl.ds(s, 2)
+        return remote(y_out_s.at[at], y_in_s.at[at], y_send.at[1, s], y_recv.at[1, s], pair)
 
     def w_copies(s, way):
         device = (2 * plane + y, t)
@@ -246,10 +254,12 @@
         def _():
             ready(s, h)
 
+        y_scale(s).start()
         for a in range(2):
-            for copy in y_copies(s + a):
-                copy.start()
-
+            y_copy(s + a).start()
+
+    def keep_half(s):
+        h = (s // 2) % 2
         for step in range(2):
             @pl.when(s == 2 * step)
             def _():
@@ -260,8 +270,12 @@
     def settle(s, sources):
         h = (s // 2) % 2
         r, f = pick(unit_r, unit_of(s)), pick(unit_f, unit_of(s))
-        for copy in y_copies(s):
-            copy.wait_recv()
+        y_copy(s).wait_recv()
+
+        @pl.when(s % 2 == 0)
+        def _():
+            y_scale(s).wait_recv()
+
         for way in range(sources):
             for copy in w_copies(s, way):
                 copy.wait_recv()
@@ -293,6 +307,8 @@
                 copy.start()
 
     turn(0, 0)
+    for copy in segments:
+        copy.wait()
     for a in range(2):
         loads[units[a][1]].wait()
         cover(*units[a], a)
@@ -306,14 +322,18 @@
 
     @pl.loop(0, count + lags[2])
     def _(i):
-        @pl.when((i < count) & (i % 2 == 0))
-        def _():
-            form(i)
-
         for sources, role in enumerate((feeder, merger, target)):
             @pl.when(role & (i >= lags[sources]) & (i < count + lags[sources]))
             def _():
                 settle(i - lags[sources], sources)
+
+        @pl.when((i < count) & (i % 2 == 0))
+        def _():
+            form(i)
+
+        @pl.when((i < count) & (i % 2 == 1))
+        def _():
+            keep_half(i - 1)
 
     blocks = [(f, h) for f in range(n_ff) for h in range(2)]
 
@@ -328,8 +348,11 @@
     @pl.loop(0, count)
     def _(s):
         r = pick(unit_r, unit_of(s))
-        for copy in y_copies(s):
-            copy.wait_send()
+        y_copy(s).wait_send()
+
+        @pl.when(s % 2 == 0)
+        def _():
+            y_scale(s).wait_send()
 
         @pl.when(z != t)
         def _():
@@ -360,13 +383,12 @@
     wide = experts * SUB
     dma = pltpu.SemaphoreType.DMA
     anywhere = pl.BlockSpec(memory_space=pl.ANY)
-    scalars = pl.BlockSpec(memory_space=pltpu.SMEM)
     data = pltpu.VMEM((count, tall, wide), jnp.int16)
     scale = pltpu.VMEM((count, 1, wide), jnp.float32)
     out = pl.pallas_call(
         functools.partial(grad_kernel, n_dp, n_t, experts),
         out_shape=jax.ShapeDtypeStruct((experts, half, ff), jnp.float32),
-        in_specs=[anywhere, anywhere, scalars, scalars],
+        in_specs=[anywhere] * 4,
         out_specs=anywhere,
         scratch_shapes=[
             pltpu.VMEM((2, 2, rows, tall), tokens.dtype),
@@ -390,6 +412,9 @@
             dma((count, experts)),
             dma((n_ff, 2, experts)),
             dma((n_ff, 2, experts)),
+            pltpu.SMEM(seg_start.shape, jnp.int32),
+            pltpu.SMEM(seg_length.shape, jnp.int32),
+            dma((2,)),
         ],
         compiler_params=pltpu.CompilerParams(
             collective_id=0, has_side_effects=True, vmem_limit_bytes=67043328

time: 97.8 us -> 96.8 us (0.990)
  Pallas kernels: 93.9 us -> 92.9 us
    pallas_call x1, Pallas kernels: 93.9 us -> 92.9 us  [kernel_device(): pl.pallas_call(functools.partial(grad_kernel, n_dp, n_t, experts), out_sh...]
where the time goes in v4:
time: 96.8 us; the launch traced here: 96.6 us
  Pallas kernels  92.9 us (96%)
  local copies, waits for them, and re-layouts  3.76 us (4%)
    pallas_call x1, Pallas kernels, kernel_device(): pl.pallas_call(functools.partial(grad_kernel, n_dp, n_t, experts), out_sh...  92.9 us
    transpose x1, local copies, waits for them, and re-layouts, kernel_device(): return out.transpose(1, 0, 2)  3.76 us

profile of v4, /device:TPU:0, one launch (start us, length us, event | category | flops | bytes accessed | tf_op | source)
XLA Modules:
  0.0 96.6 jit_solution(5115022646049891440)
XLA Ops:
  0.0 92.9 %shard_map.46 = f32[2,512,384]{2,1,0:T(8,128)} custom-call(bf16[2048,1024]{1,0:T(8,128)(2,1)} %tok_ref.1, bf16[2048,384]{1,0:T(8,128)(2,1)} %cot_ref.1, s32[1,2]{1,0:T(1,128)} %start_hbm.1, s32[1,2]{1,0:T(1,128)} %length_hbm.1), custom_call_target="tpu_custom_call" | custom-call | tf_op jit(solution)/shard_map/pallas_call | solution.py:388
  92.9 3.8 %copy.5 = f32[512,2,384]{2,1,0:T(2,128)} copy(f32[512,2,384]{2,0,1:T(8,128)} %bitcast.1) | data formatting | bytes 3145728 | tf_op jit(solution)/shard_map/transpose | solution.py:423

commit v5 on v4

--- a/solution.py
+++ b/solution.py
@@ -11,7 +11,7 @@
 SUB = 128
 STEPS = 32767.0
 TINY = 1e-30
-JOIN, MERGE, LAST = 4, 1, 3
+JOIN, MERGE, LAST = 4, 1, 2
 MESH = pl.DeviceIdType.MESH
 
 

time: 96.8 us -> 96.8 us (level)
  no operation moved by 1% of the time
where the time goes in v5:
time: 96.8 us; the launch traced here: 96.6 us
  Pallas kernels  92.9 us (96%)
  local copies, waits for them, and re-layouts  3.76 us (4%)
    pallas_call x1, Pallas kernels, kernel_device(): pl.pallas_call(functools.partial(grad_kernel, n_dp, n_t, experts), out_sh...  92.9 us
    transpose x1, local copies, waits for them, and re-layouts, kernel_device(): return out.transpose(1, 0, 2)  3.76 us

profile of v5, /device:TPU:0, one launch (start us, length us, event | category | flops | bytes accessed | tf_op | source)
XLA Modules:
  0.0 96.6 jit_solution(12996523919703083613)
XLA Ops:
  0.0 92.9 %shard_map.46 = f32[2,512,384]{2,1,0:T(8,128)} custom-call(bf16[2048,1024]{1,0:T(8,128)(2,1)} %tok_ref.1, bf16[2048,384]{1,0:T(8,128)(2,1)} %cot_ref.1, s32[1,2]{1,0:T(1,128)} %start_hbm.1, s32[1,2]{1,0:T(1,128)} %length_hbm.1), custom_call_target="tpu_custom_call" | custom-call | tf_op jit(solution)/shard_map/pallas_call | solution.py:388
  92.9 3.8 %copy.5 = f32[512,2,384]{2,1,0:T(2,128)} copy(f32[512,2,384]{2,0,1:T(8,128)} %bitcast.1) | data formatting | bytes 3145728 | tf_op jit(solution)/shard_map/transpose | solution.py:423
